TPU v7x, 32 devices: a whole 2x2x4 slice. The times are simulated.
32 devices in a mesh: graph: 2 (over x), col: 4 (over z), row: 4 (over y, core).
Axes of the slice: x: 2, y: 2, z: 4, core: 2. Of those that a mesh axis runs over, the one named last changes fastest.
Arguments:
- flow_init: float32 [16384, 8192], P(('graph', 'row'), 'col'), parts along dimension 0
- flow_graph: float32 [16384, 8192], P(('graph', 'row'), 'col'), parts along dimension 0
Outputs:
- output: float32 [16384, 8192], P(('graph', 'row'), 'col'), parts along dimension 0
There are 2 independent parts. A program takes and returns all parts, laid end to end along the dimension named above; each array names one.
All inputs are finite; a program needn't handle non-finite values.
Results may differ from a plain program's by a relative error of at most 0.001.
Values are sent between devices in bfloat16 or wider.
A program may use at most 1 GiB of HBM per device.

v0:
```python
import jax
import jax.numpy as jnp
from jax import lax
from jax.sharding import PartitionSpec as P

ITERATIONS = 3


def solution(mesh):
    num_cols = mesh.shape["col"]
    block_spec = P(("graph", "row"), "col")

    def device_step(init_blk, graph_blk):
        mat_order = init_blk.shape[1] * num_cols
        graph_panel = lax.all_gather(graph_blk.astype(jnp.bfloat16), "row", axis=0, tiled=True)
        flow_blk = init_blk
        for _ in range(ITERATIONS):
            row_panel = lax.all_gather(flow_blk.astype(jnp.bfloat16), "col", axis=1, tiled=True)
            expanded = jnp.dot(row_panel, graph_panel, preferred_element_type=jnp.float32)
            inflated = expanded * expanded
            col_sum = lax.psum(jnp.sum(inflated, axis=0), "row")
            flow_blk = inflated * (mat_order / col_sum)
        return flow_blk

    return jax.shard_map(device_step, mesh=mesh, in_specs=(block_spec, block_spec), out_specs=block_spec, check_vma=False)
```

profile of v0, /device:TPU:0, one launch (start us, length us, event | category | flops | bytes accessed | tf_op | source)
XLA Modules:
  0.0 2205.1 jit_solution(17724156792875166718)
XLA Ops:
  6.5 0.0 all-gather.5.cloned.1.call-start
  6.5 9.0 convert_element_type.12
  15.6 0.0 all-gather.5.cloned.1.call-update
  15.6 0.0 all-gather.7.cloned.1.call-start
  15.7 9.0 convert_element_type.13
  24.7 0.0 all-gather.7.cloned.1.call-update
  24.7 0.0 all-gather.9.cloned.1.call-start
  24.8 556.2 %all-gather.5.cloned.1.call-done = bf16[2048,8192]{1,0:T(8,128)(2,1)} async-done(((bf16[2048,2048]{1,0:T(8,128)(2,1)}), bf16[2048,8192]{1,0:T(8,128)(2,1)}) %all-gather.5.cloned.1.call-update) | async-done | bytes 33554448 | tf_op jit(solution)/shard_map/all_gather | solution.py:18
  580.9 201.9 %all-gather.7.cloned.1.call-done = bf16[8192,2048]{1,0:T(8,128)(2,1)} async-done(((bf16[2048,2048]{1,0:T(8,128)(2,1)}), bf16[8192,2048]{1,0:T(8,128)(2,1)}) %all-gather.7.cloned.1.call-update) | async-done | bytes 33554448 | tf_op jit(solution)/shard_map/all_gather | solution.py:15
  782.9 80.2 %multiply_reduce_fusion.2 = (f32[2048]{0:T(1024)S(1)}, f32[2048,2048]{1,0:T(8,128)}) fusion(bf16[2048,8192]{1,0:T(8,128)(2,1)} %all-gather.5.cloned.1.call-done, bf16[8192,2048]{1,0:T(8,128)(2,1)} %all-gather.7.cloned.1.call-done), kind=kOutput, calls=%fused_computation.5 | convolution fusion | flops 68727865344 | bytes 83894272 | tf_op jit(solution)/shard_map/dot_general | solution.py:19
  863.1 6.0 psum.21
  869.1 9.7 multiply_convert_fusion.1
  878.8 0.0 all-gather.9.cloned.1.call-update
  878.8 0.2 all-gather.11.cloned.1.call-start
  879.0 563.4 %all-gather.9.cloned.1.call-done = bf16[2048,8192]{1,0:T(8,128)(2,1)} async-done(((bf16[2048,2048]{1,0:T(8,128)(2,1)}), bf16[2048,8192]{1,0:T(8,128)(2,1)}) %all-gather.9.cloned.1.call-update) | async-done | bytes 33554448 | tf_op jit(solution)/shard_map/all_gather | solution.py:18
  1442.5 80.2 %multiply_reduce_fusion.1 = (f32[2048]{0:T(1024)S(1)}, f32[2048,2048]{1,0:T(8,128)}) fusion(bf16[2048,8192]{1,0:T(8,128)(2,1)} %all-gather.9.cloned.1.call-done, bf16[8192,2048]{1,0:T(8,128)(2,1)} %all-gather.7.cloned.1.call-done), kind=kOutput, calls=%fused_computation.4 | convolution fusion | flops 68727865344 | bytes 83894272 | tf_op jit(solution)/shard_map/dot_general | solution.py:19
  1522.6 7.1 psum.22
  1529.8 9.7 multiply_convert_fusion
  1539.5 0.0 all-gather.11.cloned.1.call-update
  1539.5 559.9 %all-gather.11.cloned.1.call-done = bf16[2048,8192]{1,0:T(8,128)(2,1)} async-done(((bf16[2048,2048]{1,0:T(8,128)(2,1)}), bf16[2048,8192]{1,0:T(8,128)(2,1)}) %all-gather.11.cloned.1.call-update) | async-done | bytes 33554448 | tf_op jit(solution)/shard_map/all_gather | solution.py:18
  2099.4 80.2 %multiply_reduce_fusion = (f32[2048]{0:T(1024)S(1)}, f32[2048,2048]{1,0:T(8,128)}) fusion(bf16[2048,8192]{1,0:T(8,128)(2,1)} %all-gather.11.cloned.1.call-done, bf16[8192,2048]{1,0:T(8,128)(2,1)} %all-gather.7.cloned.1.call-done), kind=kOutput, calls=%fused_computation.3 | convolution fusion | flops 68727865344 | bytes 83894272 | tf_op jit(solution)/shard_map/dot_general | solution.py:19
  2179.6 6.9 psum.23
  2186.6 12.0 multiply_multiply_fusion
  (3 shorter events, 0.0 us)
Async XLA Ops:
  6.5 574.4 %all-gather.5.cloned.1.call-start = ((), (), s32[]{:S(2)}) async-start(), calls=%async_computation | async-start | bytes 41943040 | tf_op jit(solution)/shard_map/all_gather | solution.py:18
  15.6 767.3 %all-gather.7.cloned.1.call-start = ((), (), s32[]{:S(2)}) async-start(), calls=%async_computation.1 | async-start | bytes 41943040 | tf_op jit(solution)/shard_map/all_gather | solution.py:15
  24.7 1417.7 %all-gather.9.cloned.1.call-start = ((), (), s32[]{:S(2)}) async-start(), calls=%async_computation.2 | async-start | bytes 41943040 | tf_op jit(solution)/shard_map/all_gather | solution.py:18
  878.8 1220.6 %all-gather.11.cloned.1.call-start = ((), (), s32[]{:S(2)}) async-start(), calls=%async_computation.3 | async-start | bytes 41943040 | tf_op jit(solution)/shard_map/all_gather | solution.py:18
Sparse Core Ops, SparseCore 0:
  15.7 565.1 all-gather.4
  582.5 200.3 all-gather.6
  878.9 563.4 all-gather.8
  1539.7 559.7 all-gather.10
where the time goes:
time: 2210 us
  waiting for transfers between devices  1880 us (85%)
  matrix products  241 us (11%)
  other arithmetic  49.5 us (2%)
    all_gather x3, waiting for transfers between devices, device_step(): lax.all_gather(flow_blk.astype(jnp.bfloat16), 'col', axis=1, tiled=True)  1680 us
    dot_general x3, matrix products, device_step(): jnp.dot(row_panel, graph_panel, preferred_element_type=jnp.float32)  241 us
    all_gather x1, waiting for transfers between devices, device_step(): lax.all_gather(graph_blk.astype(jnp.bfloat16), 'row', axis=0, tiled=True)  202 us
  transfers between devices with their start and end apart: 4, of which 4 were waited for; matrix products, arithmetic and copies ran while one was open for 0% of the time, Pallas kernels for 0%

commit v1 on v0

v1 whole, which is shorter than its diff:
```python
import functools

import jax
import jax.numpy as jnp
from jax import lax
from jax.experimental import pallas as pl
from jax.experimental.pallas import tpu as pltpu
from jax.sharding import PartitionSpec as P

ITERATIONS = 3
NQ = 8
MESH = pl.DeviceIdType.MESH
F32, BF16 = jnp.float32, jnp.bfloat16


def mcl_kernel(nb, mb, a_hbm, g_hbm, chome, gfull, abuf, A, C, gt, Sx, scale,
               ld_sem, st_sem, tl_sem, arecv, asend, grecv, zs, ys, ps, sr, ss, crecv, csend):
    tw = nb // NQ
    half = nb // 2
    order_n = 4 * nb
    z, i = lax.axis_index("col"), lax.axis_index("row")
    y, c = i // 2, i % 2
    side = z // 2
    mid, omid, end, oend = 1 + side, 2 - side, 3 * side, 3 - 3 * side
    is_mid = z == mid
    iy, ip = (1 - y) * 2 + c, y * 2 + (1 - c)
    iyp = (1 - y) * 2 + (1 - c)

    def rows(ii):
        return pl.ds(pl.multiple_of(ii * nb, nb), nb)

    def cols(q):
        return pl.ds(pl.multiple_of(q * tw, tw), tw)

    def halfrows(h):
        return pl.ds(pl.multiple_of(h * half, half), half)

    def gref(ii, tile):
        return gfull.at[tile, rows(ii), :]

    def gcopy(ii, tile, ssem, col, row):
        return pltpu.make_async_remote_copy(
            src_ref=gref(ii, tile), dst_ref=gref(ii, tile), send_sem=ssem, recv_sem=grecv.at[ii, tile],
            device_id={"col": col, "row": row}, device_id_type=MESH)

    def zcopy(ii, tile, s, q, col):
        return gcopy(ii, tile, zs.at[s, q], col, i)

    def ycopy(tile):
        return gcopy(i, tile, ys.at[tile], z, iy)

    def pcopy(ii, tile):
        return gcopy(ii, tile, ps.at[ii // 2, tile], z, ip)

    def gwait(ii, tile):
        gcopy(ii, tile, zs.at[0, 0], z, i).wait_recv()

    def loads(src, base, q, h):
        return pltpu.make_async_copy(src.at[halfrows(h), cols(q)], C.at[base + 2 * q + h], ld_sem.at[base + 2 * q + h])

    def each(n, body):
        def step(k, carry):
            body(k)
            return carry
        lax.fori_loop(0, n, step, 0)

    def start_loads(q):
        for h in range(2):
            loads(a_hbm, 0, q, h).start()
            loads(g_hbm, 2 * NQ, q, h).start()
    each(NQ, start_loads)

    barrier = pltpu.get_barrier_semaphore()
    me16 = z * 4 + i

    def knock(d):
        other = lax.rem(me16 + 1 + d, 16)
        pl.semaphore_signal(barrier, inc=1, device_id={"col": other // 4, "row": other % 4}, device_id_type=MESH)
    each(15, knock)
    pl.semaphore_wait(barrier, 15)

    def a_remote(q, h):
        return pltpu.make_async_remote_copy(
            src_ref=abuf.at[q, halfrows(h), :], dst_ref=A.at[:, cols(z * NQ + q)],
            send_sem=asend.at[h, q], recv_sem=arecv.at[z, q], device_id={"col": 1 + h, "row": i}, device_id_type=MESH)

    def a_local(q, h):
        return pltpu.make_async_copy(abuf.at[q, halfrows(h), :], A.at[:, cols(z * NQ + q)], arecv.at[z, q])

    def cast(src, base, q, dst):
        for h in range(2):
            loads(src, base, q, h).wait()
            gt[0, h * half:(h + 1) * half, :] = C[base + 2 * q + h].astype(BF16)
        put = pltpu.make_async_copy(gt.at[0, pl.ds(0, nb), :], dst, st_sem)
        put.start()
        put.wait()

    def hand_out(q):
        cast(a_hbm, 0, q, abuf.at[q])
        for h in range(2):
            @pl.when(z == 1 + h)
            def _():
                a_local(q, h).start()

            @pl.when(z != 1 + h)
            def _():
                a_remote(q, h).start()
        tile = z * NQ + q
        cast(g_hbm, 2 * NQ, q, gref(i, tile))
        ycopy(tile).start()

        @pl.when(is_mid)
        def _():
            pcopy(i, tile).start()
    each(NQ, hand_out)

    @pl.when(jnp.logical_not(is_mid))
    def _():
        def relay(q):
            tile = z * NQ + q
            zcopy(i, tile, 0, q, mid).start()
            gwait(iy, tile)
            zcopy(iy, tile, 1, q, mid).start()
        each(NQ, relay)

    def mtile(t):
        return jnp.where(t < NQ, omid * NQ + t, oend * NQ + t - NQ)

    def pump(t):
        @pl.when(t < 2 * NQ)
        def _():
            tm = mtile(t)
            gwait(i, tm)
            ycopy(tm).start()
            pcopy(i, tm).start()
            te = end * NQ + t // 2
            odd = t % 2

            @pl.when(odd == 0)
            def _():
                gwait(i, te)
                zcopy(i, te, 1, t // 2, omid).start()
                pcopy(i, te).start()

            @pl.when(odd == 1)
            def _():
                gwait(iy, te)
                pcopy(iy, te).start()

        @pl.when(jnp.logical_and(t >= 1, t <= 2 * NQ))
        def _():
            tm = mtile(t - 1)
            gwait(iy, tm)
            pcopy(iy, tm).start()

    me8 = (z - 1) * 4 + i

    def tile_load(tile, slot):
        return pltpu.make_async_copy(gfull.at[tile], gt.at[slot], tl_sem.at[slot])

    def compute(tile, slot, sx_slot):
        def block(m, s):
            r = pl.ds(pl.multiple_of(m * mb, mb), mb)
            acc = jnp.dot(A[r, :], gt[slot], preferred_element_type=F32)
            sq = acc * acc
            C[tile, r, :] = sq
            return s + jnp.sum(sq.reshape(mb // 8, 8, tw), axis=0)
        s = lax.fori_loop(0, half // mb, block, jnp.zeros((8, tw), F32))
        Sx[sx_slot, me8, :, cols(tile)] = jnp.sum(s, axis=0, keepdims=True)

    def s_copy(it, d):
        other = lax.rem(me8 + d, 8)
        return pltpu.make_async_remote_copy(
            src_ref=Sx.at[it, me8], dst_ref=Sx.at[it, me8], send_sem=ss.at[it, d], recv_sem=sr.at[it, me8],
            device_id={"col": 1 + other // 4, "row": other % 4}, device_id_type=MESH)

    def s_wait(it, src):
        pltpu.make_async_remote_copy(
            src_ref=Sx.at[it, src], dst_ref=Sx.at[it, src], send_sem=ss.at[it, 0], recv_sem=sr.at[it, src],
            device_id={"col": z, "row": i}, device_id_type=MESH).wait_recv()

    def renormalise(it):
        each(7, lambda d: s_copy(it, d + 1).start())
        each(7, lambda d: s_wait(it, lax.rem(me8 + d + 1, 8)))
        total = Sx[it, 0]
        for k in range(1, 8):
            total = total + Sx[it, k]
        scale[...] = float(order_n) / total

        def one(tile):
            fac = scale[:, cols(tile)]

            def part(m):
                r = pl.ds(pl.multiple_of(m * mb, mb), mb)
                A[r, cols(tile)] = (C[tile, r, :] * fac).astype(BF16)
            each(half // mb, part)
        each(4 * NQ, one)
        each(7, lambda d: s_copy(it, d + 1).wait_send())

    def order3(k):
        j = k - NQ
        both = jnp.where(j % 2 == 0, omid, end) * NQ + j // 2
        return jnp.where(k < NQ, oend * NQ + k, jnp.where(k < 3 * NQ, both, mid * NQ + k - 3 * NQ))

    def c_remote(tile):
        q = tile % NQ
        return pltpu.make_async_remote_copy(
            src_ref=C.at[tile], dst_ref=chome.at[halfrows(z - 1), cols(q)],
            send_sem=csend.at[tile], recv_sem=crecv.at[z - 1, q],
            device_id={"col": tile // NQ, "row": i}, device_id_type=MESH)

    def c_local(tile):
        q = tile % NQ
        return pltpu.make_async_copy(C.at[tile], chome.at[halfrows(z - 1), cols(q)], crecv.at[z - 1, q])

    def c_wait(h, q):
        pltpu.make_async_copy(chome.at[halfrows(h), cols(q)], chome.at[halfrows(h), cols(q)], crecv.at[h, q]).wait()

    @pl.when(is_mid)
    def _():
        def own_z(q):
            zcopy(i, z * NQ + q, 0, q, omid).start()
        each(NQ, own_z)

        def own_y(q):
            tile = z * NQ + q
            gwait(iy, tile)
            pcopy(iy, tile).start()
        each(NQ, own_y)

        def a_wait(k):
            zz, q = k // NQ, k % NQ
            pltpu.make_async_copy(abuf.at[q, halfrows(0), :], A.at[:, cols(k)], arecv.at[zz, q]).wait()
        each(4 * NQ, a_wait)

        def first(k):
            j = k - NQ
            p, r = j // 3, j % 3

            @pl.when(k == NQ // 2)
            def _():
                pump(0)

            @pl.when(k == NQ - 1)
            def _():
                pump(1)

            @pl.when(jnp.logical_and(k >= NQ, r != 1))
            def _():
                pump(2 * p + 2 + r // 2)
            tile = jnp.where(k < NQ, mid * NQ + k, jnp.where(r == 1, end * NQ + p, mtile(2 * p + r // 2)))
            gwait(ip, tile)
            gwait(iyp, tile)
            tile_load(tile, 0).start()
            tile_load(tile, 0).wait()
            compute(tile, 0, 0)
        each(4 * NQ, first)
        renormalise(0)

        def later(it):
            tile_load(order3(0), 0).start()

            def step(k):
                slot = k % 2
                tile = order3(k)
                tile_load(tile, slot).wait()

                @pl.when(k + 1 < 4 * NQ)
                def _():
                    tile_load(order3(k + 1), 1 - slot).start()
                compute(tile, slot, 1)

                @pl.when(it == 1)
                def _():
                    @pl.when(tile // NQ == z)
                    def _():
                        c_local(tile).start()

                    @pl.when(tile // NQ != z)
                    def _():
                        c_remote(tile).start()
            each(4 * NQ, step)

            @pl.when(it == 0)
            def _():
                renormalise(1)
        each(2, later)

    each(2 * NQ, lambda k: c_wait(k // NQ, k % NQ))

    def drain(q):
        tile = z * NQ + q
        ycopy(tile).wait_send()
        for h in range(2):
            @pl.when(z != 1 + h)
            def _():
                a_remote(q, h).wait_send()

        @pl.when(jnp.logical_not(is_mid))
        def _():
            zcopy(i, tile, 0, q, mid).wait_send()
            zcopy(iy, tile, 1, q, mid).wait_send()

        @pl.when(is_mid)
        def _():
            zcopy(i, tile, 0, q, omid).wait_send()
            zcopy(i, end * NQ + q, 1, q, omid).wait_send()
            ycopy(omid * NQ + q).wait_send()
            ycopy(oend * NQ + q).wait_send()
            for zz in range(4):
                pcopy(i, zz * NQ + q).wait_send()
                pcopy(iy, zz * NQ + q).wait_send()

                @pl.when(zz != z)
                def _():
                    c_remote(zz * NQ + q).wait_send()
    each(NQ, drain)


def solution(mesh):
    block_spec = P(("graph", "row"), "col")

    def device_step(init_blk, graph_blk):
        nb = init_blk.shape[1]
        n, tw = 4 * nb, nb // NQ
        mb = min(512, nb // 2)
        dma = pltpu.SemaphoreType.DMA
        any_spec = pl.BlockSpec(memory_space=pl.ANY)
        m_home, _, _ = pl.pallas_call(
            functools.partial(mcl_kernel, nb, mb),
            out_shape=(
                jax.ShapeDtypeStruct((nb, nb), F32),
                jax.ShapeDtypeStruct((4 * NQ, n, tw), BF16),
                jax.ShapeDtypeStruct((NQ, nb, tw), BF16),
            ),
            in_specs=[any_spec] * 2,
            out_specs=[any_spec] * 3,
            scratch_shapes=[
                pltpu.VMEM((nb // 2, n), BF16),
                pltpu.VMEM((4 * NQ, nb // 2, tw), F32),
                pltpu.VMEM((2, n, tw), BF16),
                pltpu.VMEM((2, 8, 1, n), F32),
                pltpu.VMEM((1, n), F32),
                dma((4 * NQ,)),
                dma(()),
                dma((2,)),
                dma((4, NQ)),
                dma((2, NQ)),
                dma((4, 4 * NQ)),
                dma((2, NQ)),
                dma((4 * NQ,)),
                dma((2, 4 * NQ)),
                dma((2, 8)),
                dma((2, 8)),
                dma((2, NQ)),
                dma((4 * NQ,)),
            ],
            compiler_params=pltpu.CompilerParams(
                collective_id=0, has_side_effects=True, vmem_limit_bytes=67043328),
            name="mcl",
        )(init_blk, graph_blk)
        col_sum = lax.psum(jnp.sum(m_home, axis=0), "row")
        return m_home * (n / col_sum)

    return jax.shard_map(device_step, mesh=mesh, in_specs=(block_spec, block_spec), out_specs=block_spec, check_vma=False)
```

time: 2210 us -> 1170 us (0.53)
  waiting for transfers between devices: 1880 us -> 0 us
  Pallas kernels: 0 us -> 1140 us
  matrix products: 241 us -> 0 us
  other arithmetic: 49.5 us -> 18.5 us
    all_gather x4 -> x0, waiting for transfers between devices: 1880 us -> none  [the longest x3 1680 us: device_step(): lax.all_gather(flow_blk.astype(jnp.bfloat16), 'col', axis=1, tiled=True)]
    pallas_call x0 -> x1, Pallas kernels: none -> 1140 us  [device_step(): pl.pallas_call(functools.partial(mcl_kernel, nb, mb), out_shape=(jax.Shap...]
    dot_general x3 -> x0, matrix products: 241 us -> none  [device_step(): jnp.dot(row_panel, graph_panel, preferred_element_type=jnp.float32)]
    convert_element_type x4 -> x0, other arithmetic: 37.5 us -> none  [the longest x3 28.5 us: device_step(): flow_blk.astype(jnp.bfloat16)]
  transfers between devices with their start and end apart: 4 -> 0, of which waited for: 4 -> 0; matrix products, arithmetic and copies ran while one was open for 0% -> 0% of each run, Pallas kernels for 0% -> 0%
where the time goes in v1:
time: 1170 us; the launch traced here: 1160 us
  Pallas kernels  1140 us (97%)
  other arithmetic  18.5 us (2%)
    pallas_call x1, Pallas kernels, device_step(): pl.pallas_call(functools.partial(mcl_kernel, nb, mb), out_shape=(jax.Shap...  1140 us

profile of v1, /device:TPU:0, one launch (start us, length us, event | category | flops | bytes accessed | tf_op | source)
XLA Modules:
  0.0 1164.8 jit_solution(11122697238850493721)
XLA Ops:
  0.0 1139.6 %mcl.1 = (f32[2048,2048]{1,0:T(8,128)}, bf16[32,8192,256]{2,1,0:T(8,128)(2,1)}, bf16[8,2048,256]{2,1,0:T(8,128)(2,1)}) custom-call(f32[2048,2048]{1,0:T(8,128)} %a_hbm.1, f32[2048,2048]{1,0:T(8,128)} %g_hbm.1), custom_call_target="tpu_custom_call" | custom-call | tf_op jit(solution)/shard_map/mcl/pallas_call | solution.py:329
  1139.6 6.6 reduce_sum.9
  1146.2 6.6 psum.7
  1152.8 11.9 %broadcast_multiply_fusion = f32[2048,2048]{1,0:T(8,128)} fusion(f32[2048,2048]{1,0:T(8,128)} %get-tuple-element.6, f32[2048]{0:T(1024)S(1)} %broadcast_divide_fusion), kind=kLoop, calls=%fused_computation | loop fusion | flops 4194304 | bytes 33562624 | tf_op jit(solution)/shard_map/mul | solution.py:363
  (1 shorter events, 0.0 us)

commit v2 on v1

v2 whole, which is shorter than its diff:
```python
import functools

import jax
import jax.numpy as jnp
from jax import lax
from jax.experimental import pallas as pl
from jax.experimental.pallas import tpu as pltpu
from jax.sharding import PartitionSpec as P

ITERATIONS = 3
NQ = 8
NS = 2
MESH = pl.DeviceIdType.MESH
F32, BF16 = jnp.float32, jnp.bfloat16


def mcl_kernel(nb, mb, a_hbm, g_hbm, chome, shome, gfull, abuf, m1b, AA, C, gt, st, Sx, scale,
               ld_sem, put_sem, tl_sem, st_sem, arecv, asend, grecv, zs, ys, ps, sr, ss, crecv, csend, hrecv, hsend):
    tw = nb // NQ
    half = nb // 2
    sub = nb // NS
    order_n = 4 * nb
    z, i = lax.axis_index("col"), lax.axis_index("row")
    y, c = i // 2, i % 2
    side = z // 2
    mid, omid, end, oend = 1 + side, 2 - side, 3 * side, 3 - 3 * side
    is_mid = z == mid
    iy, ip = (1 - y) * 2 + c, y * 2 + (1 - c)
    iyp = (1 - y) * 2 + (1 - c)

    def pos(zz):
        return jnp.where(zz == 0, 2, jnp.where(zz == 3, 3, zz - 1))

    def spos(tile):
        return pos(tile // NQ) * NQ + tile % NQ

    def cols(q):
        return pl.ds(pl.multiple_of(q * tw, tw), tw)

    def halfrows(h):
        return pl.ds(pl.multiple_of(h * half, half), half)

    def gref(ii, tile, s):
        return gfull.at[tile, pl.ds(pl.multiple_of(pos(ii) * nb + s * sub, sub), sub), :]

    def gcopy(ii, tile, s, ssem, col, row):
        return pltpu.make_async_remote_copy(
            src_ref=gref(ii, tile, s), dst_ref=gref(ii, tile, s), send_sem=ssem, recv_sem=grecv.at[ii, tile, s],
            device_id={"col": col, "row": row}, device_id_type=MESH)

    def zcopy(ii, tile, s, k, q, col):
        return gcopy(ii, tile, s, zs.at[k, q, s], col, i)

    def ycopy(tile, s):
        return gcopy(i, tile, s, ys.at[tile, s], z, iy)

    def pcopy(ii, tile, s):
        return gcopy(ii, tile, s, ps.at[ii // 2, tile, s], z, ip)

    def gwait(ii, tile, s):
        gcopy(ii, tile, s, zs.at[0, 0, 0], z, i).wait_recv()

    def loads(src, base, q, h):
        return pltpu.make_async_copy(src.at[halfrows(h), cols(q)], C.at[base + 2 * q + h], ld_sem.at[base + 2 * q + h])

    def each(n, body):
        def step(k, carry):
            body(k)
            return carry
        lax.fori_loop(0, n, step, 0)

    def start_loads(q):
        for h in range(2):
            loads(a_hbm, 0, q, h).start()
            loads(g_hbm, 2 * NQ, q, h).start()
    each(NQ, start_loads)

    barrier = pltpu.get_barrier_semaphore()
    me16 = z * 4 + i

    def knock(d):
        other = lax.rem(me16 + 1 + d, 16)
        pl.semaphore_signal(barrier, inc=1, device_id={"col": other // 4, "row": other % 4}, device_id_type=MESH)
    each(15, knock)
    pl.semaphore_wait(barrier, 15)

    def a_dst(zz, q):
        return AA.at[pos(zz) // 2, :, cols(pos(zz) % 2 * NQ + q)]

    def a_remote(q, h):
        return pltpu.make_async_remote_copy(
            src_ref=abuf.at[q, halfrows(h), :], dst_ref=a_dst(z, q),
            send_sem=asend.at[h, q], recv_sem=arecv.at[z, q], device_id={"col": 1 + h, "row": i}, device_id_type=MESH)

    def a_local(q, h):
        return pltpu.make_async_copy(abuf.at[q, halfrows(h), :], a_dst(z, q), arecv.at[z, q])

    def cast(src, base, q, dst):
        for h in range(2):
            loads(src, base, q, h).wait()
            gt[0, h * half:(h + 1) * half, :] = C[base + 2 * q + h].astype(BF16)
        put = pltpu.make_async_copy(gt.at[0, pl.ds(0, nb), :], dst, put_sem)
        put.start()
        put.wait()

    def hand_out(q):
        cast(a_hbm, 0, q, abuf.at[q])
        for h in range(2):
            @pl.when(z == 1 + h)
            def _():
                a_local(q, h).start()

            @pl.when(z != 1 + h)
            def _():
                a_remote(q, h).start()
        tile = z * NQ + q
        cast(g_hbm, 2 * NQ, q, gfull.at[tile, pl.ds(pl.multiple_of(pos(i) * nb, nb), nb), :])
        for s in range(NS):
            ycopy(tile, s).start()

            @pl.when(is_mid)
            def _():
                pcopy(i, tile, s).start()
    each(NQ, hand_out)

    @pl.when(jnp.logical_not(is_mid))
    def _():
        def relay(q):
            tile = z * NQ + q
            for s in range(NS):
                zcopy(i, tile, s, 0, q, mid).start()
            for s in range(NS):
                gwait(iy, tile, s)
                zcopy(iy, tile, s, 1, q, mid).start()
        each(NQ, relay)

    def mtile(t):
        return jnp.where(t < NQ, omid * NQ + t, oend * NQ + t - NQ)

    def pump(t):
        @pl.when(t < 2 * NQ)
        def _():
            tm = mtile(t)
            for s in range(NS):
                gwait(i, tm, s)
                ycopy(tm, s).start()
                pcopy(i, tm, s).start()
            te = end * NQ + t // 2
            odd = t % 2

            @pl.when(odd == 0)
            def _():
                for s in range(NS):
                    gwait(i, te, s)
                    zcopy(i, te, s, 1, t // 2, omid).start()
                    pcopy(i, te, s).start()

            @pl.when(odd == 1)
            def _():
                for s in range(NS):
                    gwait(iy, te, s)
                    pcopy(iy, te, s).start()

        @pl.when(jnp.logical_and(t >= 1, t <= 2 * NQ))
        def _():
            tm = mtile(t - 1)
            for s in range(NS):
                gwait(iy, tm, s)
                pcopy(iy, tm, s).start()

    me8 = (z - 1) * 4 + i

    def half_load(tile, k, slot):
        return pltpu.make_async_copy(
            gfull.at[tile, pl.ds(pl.multiple_of(k * 2 * nb, 2 * nb), 2 * nb), :], gt.at[slot], tl_sem.at[slot])

    def blocks(body):
        def step(m, s):
            return body(pl.ds(pl.multiple_of(m * mb, mb), mb), s)
        return lax.fori_loop(0, half // mb, step, jnp.zeros((8, tw), F32))

    def fold(sq):
        return jnp.sum(sq.reshape(mb // 8, 8, tw), axis=0)

    def put_sum(it, tile, s):
        Sx[it, me8, :, cols(spos(tile))] = jnp.sum(s, axis=0, keepdims=True)

    def full(it, tile, dst):
        def block(r, s):
            acc = jnp.dot(AA[0, r, :], gt[0], preferred_element_type=F32)
            acc = acc + jnp.dot(AA[1, r, :], gt[1], preferred_element_type=F32)
            sq = acc * acc
            dst[r, :] = sq
            return s + fold(sq)
        put_sum(it, tile, blocks(block))

    def first_half(tile, slot):
        def block(r, s):
            C[tile, r, :] = jnp.dot(AA[2, r, :], gt[slot], preferred_element_type=F32)
            return s
        blocks(block)

    def second_half(tile, slot):
        def block(r, s):
            acc = C[tile, r, :] + jnp.dot(AA[1, r, :], gt[slot], preferred_element_type=F32)
            sq = acc * acc
            C[tile, r, :] = sq
            return s + fold(sq)
        put_sum(1, tile, blocks(block))

    def s_copy(part, src, d):
        other = lax.rem(me8 + d, 8)
        if part < 2:
            ref = Sx.at[0, src, :, pl.ds(part * 2 * nb, 2 * nb)]
        else:
            ref = Sx.at[1, src]
        return pltpu.make_async_remote_copy(
            src_ref=ref, dst_ref=ref, send_sem=ss.at[part, d], recv_sem=sr.at[part, src],
            device_id={"col": 1 + other // 4, "row": other % 4}, device_id_type=MESH)

    def sums(part):
        each(7, lambda d: s_copy(part, me8, d + 1).start())
        each(7, lambda d: s_copy(part, lax.rem(me8 + d + 1, 8), 0).wait_recv())
        lo, n, it = (part * 2 * nb, 2 * nb, 0) if part < 2 else (0, 4 * nb, 1)
        total = Sx[it, 0, :, lo:lo + n]
        for k in range(1, 8):
            total = total + Sx[it, k, :, lo:lo + n]
        scale[:, lo:lo + n] = float(order_n) / total
        each(7, lambda d: s_copy(part, me8, d + 1).wait_send())

    def renorm(src, p, buf):
        fac = scale[:, cols(p)]

        def part(m):
            r = pl.ds(pl.multiple_of(m * mb, mb), mb)
            AA[buf, r, cols(p % (2 * NQ))] = (src[r, :] * fac).astype(BF16)
        each(half // mb, part)

    def m1_put(slot, k):
        return pltpu.make_async_copy(st.at[slot], m1b.at[k], st_sem.at[slot])

    def m1_get(slot, k):
        return pltpu.make_async_copy(m1b.at[k], st.at[slot], st_sem.at[slot])

    def order3(k):
        j = k - NQ
        both = jnp.where(j % 2 == 0, omid, end) * NQ + j // 2
        return jnp.where(k < NQ, oend * NQ + k, jnp.where(k < 3 * NQ, both, mid * NQ + k - 3 * NQ))

    def c_remote(tile):
        q = tile % NQ
        return pltpu.make_async_remote_copy(
            src_ref=C.at[tile], dst_ref=chome.at[halfrows(z - 1), cols(q)],
            send_sem=csend.at[tile], recv_sem=crecv.at[z - 1, q],
            device_id={"col": tile // NQ, "row": i}, device_id_type=MESH)

    def c_local(tile):
        q = tile % NQ
        return pltpu.make_async_copy(C.at[tile], chome.at[halfrows(z - 1), cols(q)], crecv.at[z - 1, q])

    def c_wait(h, q):
        pltpu.make_async_copy(chome.at[halfrows(h), cols(q)], chome.at[halfrows(h), cols(q)], crecv.at[h, q]).wait()

    def home_sum(k):
        zz, ii = k // 4, k % 4
        return pltpu.make_async_remote_copy(
            src_ref=Sx.at[2, me8, :, pl.ds(pl.multiple_of(pos(zz) * nb, nb), nb)], dst_ref=shome.at[me8],
            send_sem=hsend.at[k], recv_sem=hrecv.at[me8],
            device_id={"col": zz, "row": ii}, device_id_type=MESH)

    def home_sum_local():
        return pltpu.make_async_copy(
            Sx.at[2, me8, :, pl.ds(pl.multiple_of(pos(z) * nb, nb), nb)], shome.at[me8], hrecv.at[me8])

    @pl.when(is_mid)
    def _():
        def own_z(q):
            for s in range(NS):
                zcopy(i, z * NQ + q, s, 0, q, omid).start()
        each(NQ, own_z)

        def own_y(q):
            tile = z * NQ + q
            for s in range(NS):
                gwait(iy, tile, s)
                pcopy(iy, tile, s).start()
        each(NQ, own_y)

        def a_wait(k):
            zz, q = k // NQ, k % NQ
            pltpu.make_async_copy(abuf.at[q, halfrows(0), :], a_dst(zz, q), arecv.at[zz, q]).wait()
        each(4 * NQ, a_wait)

        def fetch(tile):
            for s in range(NS):
                gwait(ip, tile, s)
                gwait(iyp, tile, s)
            for k in range(2):
                half_load(tile, k, k).start()
            for k in range(2):
                half_load(tile, k, k).wait()

        def own_cols(k):
            @pl.when(k == NQ // 2)
            def _():
                pump(0)

            @pl.when(k == NQ - 1)
            def _():
                pump(1)
            tile = mid * NQ + k
            fetch(tile)
            full(0, tile, C.at[tile])
        each(NQ, own_cols)

        def advance(p, r):
            @pl.when(jnp.logical_and(r != 1, jnp.logical_or(p < NQ - 1, r == 2)))
            def _():
                pump(jnp.where(p < NQ - 1, 2 * p + 2 + r // 2, 2 * NQ))

        def tile_of(p, r):
            return jnp.where(r == 1, end * NQ + p, mtile(2 * p + r // 2))

        def b_number(tile):
            return jnp.where(tile // NQ == end, tile % NQ, NQ + tile % NQ)

        def to_stage(n, tile):
            slot = n % 2

            @pl.when(n >= 2)
            def _():
                m1_put(slot, 0).wait()
            full(0, tile, st.at[slot])
            m1_put(slot, b_number(tile)).start()

        def early(k):
            p, r = k // 3, k % 3
            advance(p, r)
            tile = tile_of(p, r)
            fetch(tile)

            @pl.when(r == 1)
            def _():
                to_stage(p, tile)

            @pl.when(r != 1)
            def _():
                full(0, tile, C.at[tile])
        each(3 * NQ // 2, early)

        sums(0)

        def renorm_a(p):
            zz = 1 + p // NQ
            renorm(C.at[zz * NQ + p % NQ], p, 2)
        each(2 * NQ, renorm_a)

        def extra(e):
            return jnp.where(e < 2 * NQ, NQ + e, end * NQ + e - 2 * NQ)

        def rest(k):
            p, r = NQ // 2 + k // 3, k % 3
            advance(p, r)
            tile = tile_of(p, r)
            fetch(tile)
            to_stage(NQ // 2 + k, tile)
            more = k < 5 * NQ // 4

            @pl.when(more)
            def _():
                half_load(extra(2 * k), 0, 1).start()

            def three(u):
                slot = u % 2

                @pl.when(u > 0)
                def _():
                    half_load(0, 0, slot).wait()

                @pl.when(u == 1)
                def _():
                    half_load(extra(2 * k + 1), 0, 0).start()
                first_half(jnp.where(u == 0, tile, extra(2 * k + u - 1)), slot)
            lax.fori_loop(0, jnp.where(more, 3, 1), lambda u, x: (three(u), x)[1], 0)
        each(3 * NQ // 2, rest)
        half_load(0, 1, 0).start()
        half_load(NQ, 1, 1).start()
        for slot in range(2):
            m1_put(slot, 0).wait()

        def b_index(p):
            zz = jnp.where(p < NQ, 0, 3)
            return b_number(zz * NQ + p % NQ)

        for slot in range(2):
            m1_get(slot, b_index(slot)).start()
        sums(1)

        def renorm_b(p):
            slot = p % 2
            m1_get(slot, 0).wait()
            renorm(st.at[slot], 2 * NQ + p, 1)

            @pl.when(p + 2 < 2 * NQ)
            def _():
                m1_get(slot, b_index(p + 2)).start()
        each(2 * NQ, renorm_b)

        def order2(k):
            return (k % 4) * NQ + k // 4

        def second(k):
            slot = k % 2
            tile = order2(k)
            half_load(tile, 1, slot).wait()
            second_half(tile, slot)

            @pl.when(k + 2 < 4 * NQ)
            def _():
                half_load(order2(k + 2), 1, slot).start()
        each(4 * NQ, second)
        for k in range(2):
            half_load(order3(0), k, k).start()
        sums(2)

        def renorm_2(p):
            pz = p // NQ
            zz = jnp.where(pz == 2, 0, jnp.where(pz == 3, 3, pz + 1))
            renorm(C.at[zz * NQ + p % NQ], p, p // (2 * NQ))
        each(4 * NQ, renorm_2)

        def third(k):
            tile = order3(k)
            for u in range(2):
                half_load(tile, u, u).wait()
            full(2, tile, C.at[tile])

            @pl.when(k + 1 < 4 * NQ)
            def _():
                for u in range(2):
                    half_load(order3(k + 1), u, u).start()

            @pl.when(tile // NQ == z)
            def _():
                c_local(tile).start()

            @pl.when(tile // NQ != z)
            def _():
                c_remote(tile).start()
        each(4 * NQ, third)

        def send_sums(k):
            @pl.when(k == me16)
            def _():
                home_sum_local().start()

            @pl.when(k != me16)
            def _():
                home_sum(k).start()
        each(16, send_sums)

    each(2 * NQ, lambda k: c_wait(k // NQ, k % NQ))
    each(8, lambda m: pltpu.make_async_copy(shome.at[m], shome.at[m], hrecv.at[m]).wait())

    def drain(q):
        tile = z * NQ + q
        for h in range(2):
            @pl.when(z != 1 + h)
            def _():
                a_remote(q, h).wait_send()
        for s in range(NS):
            ycopy(tile, s).wait_send()

            @pl.when(jnp.logical_not(is_mid))
            def _():
                zcopy(i, tile, s, 0, q, mid).wait_send()
                zcopy(iy, tile, s, 1, q, mid).wait_send()

            @pl.when(is_mid)
            def _():
                zcopy(i, tile, s, 0, q, omid).wait_send()
                zcopy(i, end * NQ + q, s, 1, q, omid).wait_send()
                ycopy(omid * NQ + q, s).wait_send()
                ycopy(oend * NQ + q, s).wait_send()
                for zz in range(4):
                    pcopy(i, zz * NQ + q, s).wait_send()
                    pcopy(iy, zz * NQ + q, s).wait_send()

        @pl.when(is_mid)
        def _():
            for zz in range(4):
                @pl.when(zz != z)
                def _():
                    c_remote(zz * NQ + q).wait_send()
            for k in range(2):
                @pl.when(2 * q + k != me16)
                def _():
                    home_sum(2 * q + k).wait_send()
    each(NQ, drain)


def solution(mesh):
    block_spec = P(("graph", "row"), "col")

    def device_step(init_blk, graph_blk):
        nb = init_blk.shape[1]
        n, tw = 4 * nb, nb // NQ
        mb = min(512, nb // 2)
        dma = pltpu.SemaphoreType.DMA
        any_spec = pl.BlockSpec(memory_space=pl.ANY)
        m_home, s_home, _, _, _ = pl.pallas_call(
            functools.partial(mcl_kernel, nb, mb),
            out_shape=(
                jax.ShapeDtypeStruct((nb, nb), F32),
                jax.ShapeDtypeStruct((8, 1, nb), F32),
                jax.ShapeDtypeStruct((4 * NQ, n, tw), BF16),
                jax.ShapeDtypeStruct((NQ, nb, tw), BF16),
                jax.ShapeDtypeStruct((2 * NQ, nb // 2, tw), F32),
            ),
            in_specs=[any_spec] * 2,
            out_specs=[any_spec] * 5,
            scratch_shapes=[
                pltpu.VMEM((3, nb // 2, 2 * nb), BF16),
                pltpu.VMEM((4 * NQ, nb // 2, tw), F32),
                pltpu.VMEM((2, 2 * nb, tw), BF16),
                pltpu.VMEM((2, nb // 2, tw), F32),
                pltpu.VMEM((3, 8, 1, n), F32),
                pltpu.VMEM((1, n), F32),
                dma((4 * NQ,)),
                dma(()),
                dma((2,)),
                dma((2,)),
                dma((4, NQ)),
                dma((2, NQ)),
                dma((4, 4 * NQ, NS)),
                dma((2, NQ, NS)),
                dma((4 * NQ, NS)),
                dma((2, 4 * NQ, NS)),
                dma((3, 8)),
                dma((3, 8)),
                dma((2, NQ)),
                dma((4 * NQ,)),
                dma((8,)),
                dma((16,)),
            ],
            compiler_params=pltpu.CompilerParams(
                collective_id=0, has_side_effects=True, vmem_limit_bytes=67043328),
            name="mcl",
        )(init_blk, graph_blk)
        col_sum = jnp.sum(s_home, axis=(0, 1))
        return m_home * (n / col_sum)

    return jax.shard_map(device_step, mesh=mesh, in_specs=(block_spec, block_spec), out_specs=block_spec, check_vma=False)
```

time: 1170 us -> 1160 us (level)
  no operation moved by 1% of the time
where the time goes in v2:
time: 1160 us
  Pallas kernels  1150 us (99%)
  other arithmetic  12.8 us (1%)
    pallas_call x1, Pallas kernels, device_step(): pl.pallas_call(functools.partial(mcl_kernel, nb, mb), out_shape=(jax.Shap...  1150 us

profile of v2, /device:TPU:0, one launch (start us, length us, event | category | flops | bytes accessed | tf_op | source)
XLA Modules:
  0.0 1161.0 jit_solution(14489455974027231445)
XLA Ops:
  0.0 1148.2 %mcl.1 = (f32[2048,2048]{1,0:T(8,128)}, f32[8,1,2048]{2,1,0:T(1,128)}, bf16[32,8192,256]{2,1,0:T(8,128)(2,1)}, bf16[8,2048,256]{2,1,0:T(8,128)(2,1)}, f32[16,1024,256]{2,1,0:T(8,128)}) custom-call(f32[2048,2048]{1,0:T(8,128)} %a_hbm.1, f32[2048,2048]{1,0:T(8,128)} %g_hbm.1), custom_call_target="tpu_custom_call" | custom-call | tf_op jit(solution)/shard_map/mcl/pallas_call | solution.py:511
  1148.2 0.9 reduce_sum.9
  1149.1 11.9 %broadcast_multiply_fusion = f32[2048,2048]{1,0:T(8,128)} fusion(f32[2048,2048]{1,0:T(8,128)} %get-tuple-element.7, f32[2048]{0:T(1024)S(1)} %broadcast_divide_fusion), kind=kLoop, calls=%fused_computation | loop fusion | flops 4194304 | bytes 33562624 | tf_op jit(solution)/shard_map/mul | solution.py:551
  (1 shorter events, 0.0 us)
